TPU v7x, 32 devices: a whole 2x2x4 slice. The times are simulated.
32 devices in a mesh: grp: 2 (over x), ep: 16 (over z, y, core).
Axes of the slice: x: 2, y: 2, z: 4, core: 2. Of those that a mesh axis runs over, the one named last changes fastest.
Arguments:
- expert_ids: int32 [2048, 8], P(('grp', 'ep')), parts along dimension 0, may hold values from 0 to 15, all different within a row; in each aligned block of 64 rows (0 to 63, 64 to 127, ...) at most 64 rows name the same one
- route_gates: float32 [2048, 8], P(('grp', 'ep')), parts along dimension 0, may hold values from 0.1 to 0.5
- routed_in: bfloat16 [2048, 8, 2048], P(('grp', 'ep')), parts along dimension 0, may hold values from -6 to 6
- down_weight: bfloat16 [16, 1024, 3584], P('ep'), may hold values from -0.1875 to 0.1875
- slot_offset: int32 [1], replicated, may hold values from 0 to 15
Outputs:
- combined: bfloat16 [2048, 3584], P(('grp', 'ep')), parts along dimension 0
There are 2 independent parts, one for each index of `grp`. A program takes and returns all parts, laid end to end along the dimension named above; an argument that names none is the same for every part. Nothing has to cross between parts.
Inputs may be any that keep to these rules, and one draw needn't show every extreme that they name: `expert_ids`: each row names 8 different experts. Among the tokens of one ep device, no expert is named by more than 64 tokens, a bound that some block reaches in some devices.
All inputs are finite; a program needn't handle non-finite values.
Results may differ from a plain program's by a relative error of at most 0.0057.
Values may be sent and summed in bfloat16 or wider, within the bound.
A program may use at most 128 MiB of HBM per device.

v0:
```python
import jax
import jax.numpy as jnp
from jax import lax
from jax.sharding import PartitionSpec as P


def swiglu(packed):
    half = packed.shape[-1] // 2
    gate = packed[..., :half].astype(jnp.float32)
    upper = packed[..., half:].astype(jnp.float32)
    return (jax.nn.silu(gate) * upper).astype(jnp.bfloat16)


def on_device(expert_ids, route_gates, routed_in, down_weight, slot_offset):
    experts = lax.axis_size("ep")
    tokens_here, chosen = expert_ids.shape
    pair_count = tokens_here * chosen
    capacity = 2 * pair_count // experts
    matrix = down_weight[0]
    offset = slot_offset[0]
    target = jnp.mod(expert_ids.reshape(pair_count) - offset, experts)
    onehot = (target[:, None] == jnp.arange(experts, dtype=jnp.int32)[None, :]).astype(jnp.int32)
    earlier = jnp.cumsum(onehot, axis=0) - onehot
    rank = jnp.sum(earlier * onehot, axis=1)
    row_index = target * capacity + rank
    source = (
        jnp.full((experts * capacity,), pair_count, jnp.int32)
        .at[row_index]
        .set(jnp.arange(pair_count, dtype=jnp.int32))
    )
    payload = routed_in.reshape(pair_count, routed_in.shape[2])
    payload = swiglu(payload)
    padded = jnp.concatenate([payload, jnp.zeros((1, payload.shape[1]), jnp.bfloat16)], axis=0)
    outgoing = jnp.take(padded, source, axis=0).reshape(experts, capacity, payload.shape[1])
    results = jnp.einsum(
        "nkf,fd->nkd",
        lax.all_to_all(outgoing, "ep", split_axis=0, concat_axis=0, tiled=True),
        matrix,
        preferred_element_type=jnp.float32,
    ).astype(jnp.bfloat16)
    returned = lax.all_to_all(results, "ep", split_axis=0, concat_axis=0, tiled=True)
    width = returned.shape[2]
    picked = jnp.take(returned.reshape(experts * capacity, width), row_index, axis=0).reshape(
        tokens_here, chosen, width
    )
    total = jnp.zeros((tokens_here, width), jnp.float32)
    for choice_index in range(chosen):
        total = total + route_gates[:, choice_index, None] * picked[:, choice_index].astype(
            jnp.float32
        )
    return total.astype(jnp.bfloat16)


def solution(mesh):
    placed = (
        P(("grp", "ep"), None),
        P(("grp", "ep"), None),
        P(("grp", "ep"), None, None),
        P("ep", None, None),
        P(),
    )
    return jax.shard_map(
        on_device, mesh=mesh, in_specs=placed, out_specs=P(("grp", "ep"), None), check_vma=False
    )
```

profile of v0, /device:TPU:13, one launch (start us, length us, event | category | flops | bytes accessed | tf_op | source)
XLA Modules:
  0.0 262.0 jit_solution(6302886121421381690)
XLA Ops:
  0.7 0.7 broadcast_subtract_fusion
  1.3 0.1 copy.11
  1.4 0.1 sub.35
  1.5 0.1 sub.34
  1.6 0.1 sub.37
  1.7 1.2 reduce-window.6
  2.9 0.2 slice_reduce_fusion
  3.2 0.1 fusion.16
  3.3 2.4 scatter_custom_fusion
  5.8 2.2 fusion.5
  8.0 0.1 broadcast_in_dim.33
  8.1 0.1 concatenate.3
  8.1 4.1 %gather_fusion = bf16[1024,1024]{1,0:T(8,128)(2,1)S(1)} fusion(bf16[513,1024]{1,0:T(8,128)(2,1)S(1)} %concatenate.3, s32[1024]{0:T(1024)S(1)} %fusion.21), kind=kCustom, calls=%fused_computation | custom fusion | bytes 4198400 | tf_op jit(solution)/shard_map/jit(_take)/gather | solution.py:34
  12.2 0.3 broadcast_select_fusion
  12.5 53.6 %all_to_all.10 = bf16[16,64,1024]{2,1,0:T(8,128)(2,1)S(1)} all-to-all(bf16[16,64,1024]{2,1,0:T(8,128)(2,1)S(1)} %broadcast_select_fusion), channel_id=1, replica_groups=mesh['grp'=2,'ep'=16] {'ep'}, dimensions={0} | all-to-all | bytes 4194304 | tf_op jit(solution)/shard_map/all_to_all | solution.py:37
  66.1 12.8 %convolution_convert_fusion = bf16[16,64,3584]{2,1,0:T(8,128)(2,1)} fusion(bf16[16,64,1024]{2,1,0:T(8,128)(2,1)S(1)} %all_to_all.10, bf16[1,1024,3584]{2,1,0:T(8,128)(2,1)} %param.8), kind=kOutput, calls=%fused_computation.3 | convolution fusion | flops 7519862784 | bytes 16777216 | tf_op jit(solution)/shard_map/nkf,fd->nkd/dot_general | solution.py:35
  78.9 0.0 copy-start.1
  78.9 0.0 copy-start
  78.9 5.2 %all-to-all-start.1 = ((bf16[16,64,3584]{2,1,0:T(8,128)(2,1)}), bf16[16,64,3584]{2,1,0:T(8,128)(2,1)}, u32[]{:S(2)}, u32[]{:S(2)}) async-start(bf16[16,64,3584]{2,1,0:T(8,128)(2,1)} %convolution_convert_fusion), calls=%async_computation.1 | async-start | bytes 14680064 | tf_op jit(solution)/shard_map/all_to_all | solution.py:41
  84.1 0.1 reduce_sum.14
  84.2 0.1 copy.14
  84.3 0.0 copy-done.1
  84.3 0.0 copy-done
  84.3 159.7 %all-to-all-done.1 = bf16[16,64,3584]{2,1,0:T(8,128)(2,1)} async-done(((bf16[16,64,3584]{2,1,0:T(8,128)(2,1)}), bf16[16,64,3584]{2,1,0:T(8,128)(2,1)}, u32[]{:S(2)}, u32[]{:S(2)}) %all-to-all-start.1) | async-done | bytes 7340064 | tf_op jit(solution)/shard_map/all_to_all | solution.py:41
  244.0 11.9 %gather_fusion.1 = bf16[512,3584]{1,0:T(8,128)(2,1)} fusion(bf16[1024,3584]{1,0:T(8,128)(2,1)} %bitcast.9, s32[1024]{0:T(1024)S(1)} %pad_clamp_fusion), kind=kCustom, calls=%fused_computation.1 | custom fusion | bytes 7342080 | tf_op jit(solution)/shard_map/jit(_take)/gather | solution.py:43
  255.9 4.4 %copy_select_fusion = bf16[64,8,3584]{2,0,1:T(8,128)(2,1)S(1)} fusion(bf16[64,8,3584]{2,1,0:T(8,128)(2,1)} %bitcast.89, pred[64,8]{0,1:T(8,128)(4,1)S(1)} %compare_and_fusion.1), kind=kLoop, calls=%fused_computation.5 | loop fusion | flops 1835008 | bytes 7340544 | tf_op jit(solution)/shard_map/jit(_take)/select_n | solution.py:43
  260.3 1.7 fusion.7
  (12 shorter events, 0.1 us)
Async XLA Ops:
  78.9 5.3 %copy-start.1 = (f32[64,8]{0,1:T(8,128)S(1)}, f32[64,8]{0,1:T(8,128)}, u32[]{:S(2)}) copy-start(f32[64,8]{0,1:T(8,128)} %param.6) | copy-start | bytes 6148
  78.9 5.3 %copy-start = (s32[64,8]{0,1:T(8,128)S(1)}, s32[64,8]{0,1:T(8,128)}, u32[]{:S(2)}) copy-start(s32[64,8]{0,1:T(8,128)} %param.5) | copy-start | bytes 6148
  78.9 165.0 %all-to-all-start.1 = ((bf16[16,64,3584]{2,1,0:T(8,128)(2,1)}), bf16[16,64,3584]{2,1,0:T(8,128)(2,1)}, u32[]{:S(2)}, u32[]{:S(2)}) async-start(bf16[16,64,3584]{2,1,0:T(8,128)(2,1)} %convolution_convert_fusion), calls=%async_computation.1 | async-start | bytes 14680064 | tf_op jit(solution)/shard_map/all_to_all | solution.py:41
where the time goes:
time: 262 us
  waiting for transfers between devices  160 us (61%)
  blocking collectives  53.6 us (20%)
  local copies, waits for them, and re-layouts  19.3 us (7%)
  matrix products  12.8 us (5%)
  other arithmetic  10.6 us (4%)
  starting transfers between devices  5.16 us (2%)
    all_to_all x1, waiting for transfers between devices, on_device(): lax.all_to_all(results, 'ep', split_axis=0, concat_axis=0, tiled=True)  160 us
    all_to_all x1, blocking collectives, on_device(): lax.all_to_all(outgoing, 'ep', split_axis=0, concat_axis=0, tiled=True)  53.6 us
    dot_general x1, matrix products, on_device(): jnp.einsum('nkf,fd->nkd', lax.all_to_all(outgoing, 'ep', split_axis=0, co...  12.8 us
    gather x1, local copies, waits for them, and re-layouts, on_device(): jnp.take(returned.reshape(experts * capacity, width), row_index, axis=0)  11.9 us
  transfers between devices with their start and end apart: 1, of which 1 were waited for; matrix products, arithmetic and copies ran while one was open for 0% of the time, Pallas kernels for 0%

commit v1 on v0

--- a/solution.py
+++ b/solution.py
@@ -1,7 +1,16 @@
+import functools
+
 import jax
 import jax.numpy as jnp
 from jax import lax
+from jax.experimental import pallas as pl
+from jax.experimental.pallas import tpu as pltpu
 from jax.sharding import PartitionSpec as P
+
+MESH = pl.DeviceIdType.MESH
+TILE = 256
+HALVES = 2
+VMEM_LIMIT = 63 * 1024 * 1024
 
 
 def swiglu(packed):
@@ -11,7 +20,7 @@
     return (jax.nn.silu(gate) * upper).astype(jnp.bfloat16)
 
 
-def on_device(expert_ids, route_gates, routed_in, down_weight, slot_offset):
+def exchange_form(expert_ids, route_gates, routed_in, down_weight, slot_offset):
     experts = lax.axis_size("ep")
     tokens_here, chosen = expert_ids.shape
     pair_count = tokens_here * chosen
@@ -28,8 +37,7 @@
         .at[row_index]
         .set(jnp.arange(pair_count, dtype=jnp.int32))
     )
-    payload = routed_in.reshape(pair_count, routed_in.shape[2])
-    payload = swiglu(payload)
+    payload = swiglu(routed_in.reshape(pair_count, routed_in.shape[2]))
     padded = jnp.concatenate([payload, jnp.zeros((1, payload.shape[1]), jnp.bfloat16)], axis=0)
     outgoing = jnp.take(padded, source, axis=0).reshape(experts, capacity, payload.shape[1])
     results = jnp.einsum(
@@ -51,6 +59,255 @@
     return total.astype(jnp.bfloat16)
 
 
+def flipped(index, distance):
+    result, bit = index, 1
+    while bit <= distance:
+        if distance & bit:
+            result = result + bit - 2 * bit * lax.rem(lax.div(index, bit), 2)
+        bit *= 2
+    return result
+
+
+def slot_distance(group, slot):
+    return group * 4 + (slot % 2) * 2 + slot // 2
+
+
+def kernel(
+    n,
+    target_ref,
+    gate_ref,
+    x_hbm,
+    w_hbm,
+    out_ref,
+    x,
+    w,
+    hid,
+    outg,
+    recv,
+    own,
+    psend,
+    crecv,
+    ysend,
+    yrecv,
+    zsend,
+    zrecv,
+    lsem,
+    dsend_sem,
+    drecv_sem,
+    csend_sem,
+    crecv_sem,
+    ysend_sem,
+    yrecv_sem,
+    zsend_sem,
+    zrecv_sem,
+):
+    me = lax.axis_index("ep")
+    tokens, chosen = target_ref.shape
+    pairs = tokens * chosen
+    features = hid.shape[1]
+    groups, halves, _, wide = own.shape
+
+    barrier = pltpu.get_barrier_semaphore()
+    for d in range(1, n):
+        pl.semaphore_signal(barrier, inc=1, device_id={"ep": flipped(me, d)}, device_id_type=MESH)
+    x_copy = pltpu.make_async_copy(x_hbm, x, lsem.at[0])
+    x_copy.start()
+    w_copy = pltpu.make_async_copy(w_hbm.at[0], w, lsem.at[1])
+    w_copy.start()
+    x_copy.wait()
+
+    @pl.loop(0, tokens // 8)
+    def _(block):
+        rows = x[pl.ds(pl.multiple_of(block * 8, 8), 8)].astype(jnp.float32)
+        rows = rows.reshape(8 * chosen, 2 * features)
+        value = jax.nn.silu(rows[:, :features]) * rows[:, features:]
+        start = pl.multiple_of(block * 8 * chosen, 8 * chosen)
+        hid[pl.ds(start, 8 * chosen)] = value.astype(jnp.bfloat16)
+
+    pl.semaphore_wait(barrier, n - 1)
+
+    target = target_ref[...]
+    gates = gate_ref[...]
+    lane = lax.broadcasted_iota(jnp.int32, (chosen, pairs), 1)
+    spread = (lane % chosen == lax.broadcasted_iota(jnp.int32, (chosen, pairs), 0)).astype(jnp.bfloat16)
+    mine = (
+        lax.broadcasted_iota(jnp.int32, (tokens, pairs), 1) // chosen
+        == lax.broadcasted_iota(jnp.int32, (tokens, pairs), 0)
+    )
+    order = list(range(groups - 1, -1, -1))
+    dispatch = {}
+    for g in order:
+        picks, scales = [], []
+        for q in range(4):
+            hit = target == flipped(me, slot_distance(g, q))
+            scales.append(jnp.sum(jnp.where(hit, gates, 0.0), axis=1, keepdims=True))
+            chosen_here = jnp.dot(
+                hit.astype(jnp.float32).astype(jnp.bfloat16), spread, preferred_element_type=jnp.float32
+            )
+            picks.append(jnp.where(mine, chosen_here, 0.0).astype(jnp.bfloat16))
+        pick = jnp.concatenate(picks, axis=0)
+        scale = jnp.concatenate(scales, axis=0)
+        for c in range(0, features, TILE):
+            rows = jnp.dot(pick, hid[:, c : c + TILE], preferred_element_type=jnp.float32)
+            rows = (rows * scale).astype(jnp.bfloat16)
+            if g == 0:
+                recv[0, 0:tokens, c : c + TILE] = rows[0:tokens]
+                outg[0, tokens:, c : c + TILE] = rows[tokens:]
+            else:
+                outg[g, :, c : c + TILE] = rows
+        for q in range(4):
+            d = slot_distance(g, q)
+            if d == 0:
+                continue
+            dispatch[d] = pltpu.make_async_remote_copy(
+                src_ref=outg.at[g, pl.ds(q * tokens, tokens)],
+                dst_ref=recv.at[g, pl.ds(q * tokens, tokens)],
+                send_sem=dsend_sem.at[d],
+                recv_sem=drecv_sem.at[d],
+                device_id={"ep": flipped(me, d)},
+                device_id_type=MESH,
+            )
+            dispatch[d].start()
+    w_copy.wait()
+
+    core, side, far = {}, {}, {}
+
+    def finish_core(g, h):
+        core[g, h].wait_recv()
+        own[g, h, 0:tokens] = own[g, h, 0:tokens] + crecv[g, h, 0:tokens].astype(jnp.float32)
+        ysend[g, h] = (own[g, h, tokens:] + crecv[g, h, tokens:].astype(jnp.float32)).astype(jnp.bfloat16)
+        side[g, h] = pltpu.make_async_remote_copy(
+            src_ref=ysend.at[g, h],
+            dst_ref=yrecv.at[g, h],
+            send_sem=ysend_sem.at[g, h],
+            recv_sem=yrecv_sem.at[g, h],
+            device_id={"ep": flipped(me, 2)},
+            device_id_type=MESH,
+        )
+        side[g, h].start()
+
+    def finish_side(g, h):
+        side[g, h].wait_recv()
+        value = own[g, h, 0:tokens] + yrecv[g, h].astype(jnp.float32)
+        if g == 0:
+            own[g, h, 0:tokens] = value
+            return
+        zsend[g - 1, h] = value.astype(jnp.bfloat16)
+        far[g, h] = pltpu.make_async_remote_copy(
+            src_ref=zsend.at[g - 1, h],
+            dst_ref=zrecv.at[g - 1, h],
+            send_sem=zsend_sem.at[g - 1, h],
+            recv_sem=zrecv_sem.at[g - 1, h],
+            device_id={"ep": flipped(me, 4 * g)},
+            device_id_type=MESH,
+        )
+        far[g, h].start()
+
+    for place, g in enumerate(order):
+        for q in range(4):
+            if slot_distance(g, q):
+                dispatch[slot_distance(g, q)].wait_recv()
+        for h in range(halves):
+
+            @pl.loop(0, wide // TILE)
+            def _(j):
+                here = pl.ds(pl.multiple_of(j * TILE, TILE), TILE)
+                there = pl.ds(pl.multiple_of(h * wide + j * TILE, TILE), TILE)
+                result = jnp.dot(recv[g], w[:, there], preferred_element_type=jnp.float32)
+                own[g, h, :, here] = result[: 2 * tokens]
+                psend[g, h, :, here] = result[2 * tokens :].astype(jnp.bfloat16)
+
+            core[g, h] = pltpu.make_async_remote_copy(
+                src_ref=psend.at[g, h],
+                dst_ref=crecv.at[g, h],
+                send_sem=csend_sem.at[g, h],
+                recv_sem=crecv_sem.at[g, h],
+                device_id={"ep": flipped(me, 1)},
+                device_id_type=MESH,
+            )
+            core[g, h].start()
+        for h in range(halves):
+            finish_core(g, h)
+        if place:
+            for h in range(halves):
+                finish_side(order[place - 1], h)
+    for h in range(halves):
+        finish_side(0, h)
+    for h in range(halves):
+        total = own[0, h, 0:tokens]
+        for g in order[:-1]:
+            far[g, h].wait_recv()
+            total = total + zrecv[g - 1, h].astype(jnp.float32)
+        out_ref[:, h * wide : (h + 1) * wide] = total.astype(jnp.bfloat16)
+    for copies in (dispatch, core, side, far):
+        for copy in copies.values():
+            copy.wait_send()
+
+
+def scratch_of(n, tokens, chosen, features, width):
+    groups, wide = n // 4, width // HALVES
+    small = jnp.bfloat16
+    return [
+        ((tokens, chosen, 2 * features), small),
+        ((features, width), small),
+        ((tokens * chosen, features), small),
+        ((groups, 4 * tokens, features), small),
+        ((groups, 4 * tokens, features), small),
+        ((groups, HALVES, 2 * tokens, wide), jnp.float32),
+        ((groups, HALVES, 2 * tokens, wide), small),
+        ((groups, HALVES, 2 * tokens, wide), small),
+        ((groups, HALVES, tokens, wide), small),
+        ((groups, HALVES, tokens, wide), small),
+        ((max(groups - 1, 1), HALVES, tokens, wide), small),
+        ((max(groups - 1, 1), HALVES, tokens, wide), small),
+    ]
+
+
+def bytes_of(buffers):
+    total = 0
+    for shape, kind in buffers:
+        size = jnp.dtype(kind).itemsize
+        for extent in shape:
+            size *= extent
+        total += size
+    return total
+
+
+def on_device(expert_ids, route_gates, routed_in, down_weight, slot_offset):
+    n = lax.axis_size("ep")
+    tokens, chosen = expert_ids.shape
+    features, width = down_weight.shape[1:]
+    buffers = scratch_of(n, tokens, chosen, features, width)
+    if (
+        n < 4
+        or n & (n - 1)
+        or tokens % 16
+        or chosen % 8
+        or features % TILE
+        or width % (HALVES * TILE)
+        or bytes_of(buffers) > VMEM_LIMIT * 3 // 4
+    ):
+        return exchange_form(expert_ids, route_gates, routed_in, down_weight, slot_offset)
+    groups = n // 4
+    target = jnp.mod(expert_ids - slot_offset[0], n)
+    dma = pltpu.SemaphoreType.DMA
+    pair = (groups, HALVES)
+    far = (max(groups - 1, 1), HALVES)
+    return pl.pallas_call(
+        functools.partial(kernel, n),
+        out_shape=jax.ShapeDtypeStruct((tokens, width), jnp.bfloat16),
+        in_specs=[pl.BlockSpec(memory_space=pltpu.VMEM)] * 2 + [pl.BlockSpec(memory_space=pl.ANY)] * 2,
+        out_specs=pl.BlockSpec(memory_space=pltpu.VMEM),
+        scratch_shapes=[pltpu.VMEM(shape, kind) for shape, kind in buffers]
+        + [dma((2,)), dma((n,)), dma((n,))]
+        + [dma(pair)] * 4
+        + [dma(far)] * 2,
+        compiler_params=pltpu.CompilerParams(
+            collective_id=0, has_side_effects=True, vmem_limit_bytes=VMEM_LIMIT
+        ),
+    )(target, route_gates, routed_in, down_weight)
+
+
 def solution(mesh):
     placed = (
         P(("grp", "ep"), None),

time: 262 us -> 106 us (0.40)
  the two profiles are of different devices: /device:TPU:13 before, /device:TPU:0 now
where the time goes in v1:
time: 106 us; the launch traced here: 105 us
  Pallas kernels  100 us (94%)
  local copies, waits for them, and re-layouts  3.96 us (4%)
    pallas_call x1, Pallas kernels, on_device(): pl.pallas_call(functools.partial(kernel, n), out_shape=jax.ShapeDtypeStru...  100 us
    unnamed x3, local copies, waits for them, and re-layouts  3.96 us

profile of v1, /device:TPU:0, one launch (start us, length us, event | category | flops | bytes accessed | tf_op | source)
XLA Modules:
  0.0 105.3 jit_solution(14143648121384179499)
XLA Ops:
  0.7 0.8 copy.6
  1.4 0.6 add_select_fusion.target_ref
  2.1 1.4 %copy.7.gate_ref = f32[64,8]{1,0:T(8,128)} copy(f32[64,8]{0,1:T(8,128)} %param.6) | data formatting | bytes 4096 | tf_op args[1]
  3.4 100.0 %shard_map.55 = bf16[64,3584]{1,0:T(8,128)(2,1)} custom-call(s32[64,8]{1,0:T(8,128)} %add_select_fusion.target_ref, f32[64,8]{1,0:T(8,128)} %copy.7.gate_ref, bf16[64,8,2048]{2,1,0:T(8,128)(2,1)} %x_hbm.1, bf16[1,1024,3584]{2,1,0:T(8,128)(2,1)} %w_hbm.1), custom_call_target="tpu_custom_call" | custom-call | tf_op jit(solution)/shard_map/pallas_call | solution.py:296
  103.5 1.8 %copy.10 = bf16[64,3584]{1,0:T(8,128)(2,1)} copy(bf16[64,3584]{1,0:T(8,128)(2,1)} %shard_map.55) | data formatting | bytes 917504

commit v2 on v0

--- a/solution.py
+++ b/solution.py
@@ -1,7 +1,16 @@
+import functools
+
 import jax
 import jax.numpy as jnp
 from jax import lax
+from jax.experimental import pallas as pl
+from jax.experimental.pallas import tpu as pltpu
 from jax.sharding import PartitionSpec as P
+
+MESH = pl.DeviceIdType.MESH
+TILE = 256
+CHUNKS = 4
+VMEM_LIMIT = 63 * 1024 * 1024
 
 
 def swiglu(packed):
@@ -11,7 +20,7 @@
     return (jax.nn.silu(gate) * upper).astype(jnp.bfloat16)
 
 
-def on_device(expert_ids, route_gates, routed_in, down_weight, slot_offset):
+def exchange_form(expert_ids, route_gates, routed_in, down_weight, slot_offset):
     experts = lax.axis_size("ep")
     tokens_here, chosen = expert_ids.shape
     pair_count = tokens_here * chosen
@@ -28,8 +37,7 @@
         .at[row_index]
         .set(jnp.arange(pair_count, dtype=jnp.int32))
     )
-    payload = routed_in.reshape(pair_count, routed_in.shape[2])
-    payload = swiglu(payload)
+    payload = swiglu(routed_in.reshape(pair_count, routed_in.shape[2]))
     padded = jnp.concatenate([payload, jnp.zeros((1, payload.shape[1]), jnp.bfloat16)], axis=0)
     outgoing = jnp.take(padded, source, axis=0).reshape(experts, capacity, payload.shape[1])
     results = jnp.einsum(
@@ -51,6 +59,254 @@
     return total.astype(jnp.bfloat16)
 
 
+def flipped(index, distance):
+    result, bit = index, 1
+    while bit <= distance:
+        if distance & bit:
+            result = result + bit - 2 * bit * lax.rem(lax.div(index, bit), 2)
+        bit *= 2
+    return result
+
+
+def slot_distance(n, slot):
+    groups = n // 4
+    return (groups - 1 - slot % groups) * 4 + (slot // groups % 2) * 2 + slot // (2 * groups)
+
+
+def kernel(
+    n,
+    target_ref,
+    gate_ref,
+    x_hbm,
+    w_hbm,
+    out_ref,
+    x,
+    w,
+    outg,
+    recv,
+    own,
+    psend,
+    crecv,
+    ysend,
+    yrecv,
+    zsend,
+    zrecv,
+    wsem,
+    xsem,
+    dsend_sem,
+    drecv_sem,
+    csend_sem,
+    crecv_sem,
+    ysend_sem,
+    yrecv_sem,
+    zsend_sem,
+    zrecv_sem,
+):
+    me = lax.axis_index("ep")
+    chosen = target_ref.shape[1]
+    features, width = w.shape
+    chunks, rows_all, _ = recv.shape
+    part = rows_all // n
+    pairs = part * chosen
+    groups = n // 4
+    plane = groups * part
+
+    def send(src, dst, send_sem, recv_sem, distance):
+        copy = pltpu.make_async_remote_copy(
+            src_ref=src,
+            dst_ref=dst,
+            send_sem=send_sem,
+            recv_sem=recv_sem,
+            device_id={"ep": flipped(me, distance)},
+            device_id_type=MESH,
+        )
+        copy.start()
+        return copy
+
+    barrier = pltpu.get_barrier_semaphore()
+    for d in range(1, n):
+        pl.semaphore_signal(barrier, inc=1, device_id={"ep": flipped(me, d)}, device_id_type=MESH)
+    x_copies = []
+    for k in range(chunks):
+        tokens_of = pl.ds(k * part, part)
+        x_copies.append(pltpu.make_async_copy(x_hbm.at[tokens_of], x.at[tokens_of], xsem.at[k]))
+        x_copies[k].start()
+    w_copy = pltpu.make_async_copy(w_hbm.at[0], w, wsem.at[0])
+    w_copy.start()
+
+    lane = lax.broadcasted_iota(jnp.int32, (chosen, pairs), 1)
+    spread = (lane % chosen == lax.broadcasted_iota(jnp.int32, (chosen, pairs), 0)).astype(jnp.bfloat16)
+    mine = (
+        lax.broadcasted_iota(jnp.int32, (rows_all, pairs), 1) // chosen
+        == lax.broadcasted_iota(jnp.int32, (rows_all, pairs), 0) % part
+    )
+    slots = [slot_distance(n, s) for s in range(n)]
+    peers = [flipped(me, d) for d in slots]
+    dispatch = {}
+    for k in range(chunks):
+        target = target_ref[k * part : (k + 1) * part]
+        gates = gate_ref[k * part : (k + 1) * part]
+        hit = jnp.concatenate([jnp.where(target == e, 1.0, 0.0) for e in peers], axis=0)
+        scale = jnp.sum(hit * jnp.concatenate([gates] * n, axis=0), axis=1, keepdims=True)
+        wanted = jnp.dot(hit.astype(jnp.bfloat16), spread, preferred_element_type=jnp.float32)
+        pick = jnp.where(mine, wanted, 0.0).astype(jnp.bfloat16)
+        x_copies[k].wait()
+        for c in range(0, features, TILE):
+            gate = x[k * part : (k + 1) * part, :, c : c + TILE].astype(jnp.float32)
+            upper = x[k * part : (k + 1) * part, :, features + c : features + c + TILE].astype(jnp.float32)
+            hidden = (jax.nn.silu(gate) * upper).reshape(pairs, TILE).astype(jnp.bfloat16)
+            rows = jnp.dot(pick, hidden, preferred_element_type=jnp.float32)
+            rows = (rows * scale).astype(jnp.bfloat16)
+            for s, d in enumerate(slots):
+                if d:
+                    outg[k, s * part : (s + 1) * part, c : c + TILE] = rows[s * part : (s + 1) * part]
+                else:
+                    recv[k, s * part : (s + 1) * part, c : c + TILE] = rows[s * part : (s + 1) * part]
+        if k == 0:
+            pl.semaphore_wait(barrier, n - 1)
+        for d in range(n - 1, 0, -1):
+            s = slots.index(d)
+            here = pl.ds(s * part, part)
+            dispatch[k, s] = send(
+                outg.at[k, here], recv.at[k, here], dsend_sem.at[k, s], drecv_sem.at[k, s], d
+            )
+    w_copy.wait()
+
+    core, side, line = {}, {}, {}
+
+    def row_of(dz):
+        return pl.ds((groups - 1 - dz) * part, part)
+
+    def multiply(k):
+        for s, d in enumerate(slots):
+            if d:
+                dispatch[k, s].wait_recv()
+
+        @pl.loop(0, width // TILE)
+        def _(j):
+            here = pl.ds(pl.multiple_of(j * TILE, TILE), TILE)
+            result = jnp.dot(recv[k], w[:, here], preferred_element_type=jnp.float32)
+            own[k, :, here] = result[: 2 * plane]
+            psend[k, :, here] = result[2 * plane :].astype(jnp.bfloat16)
+
+        core[k] = send(psend.at[k], crecv.at[k], csend_sem.at[k], crecv_sem.at[k], 1)
+
+    def finish_core(k):
+        core[k].wait_recv()
+        for p in range(2):
+            here = pl.ds(p * plane // 2, plane // 2)
+            there = pl.ds(plane + p * plane // 2, plane // 2)
+            ysend[k, here] = (own[k, there] + crecv[k, there].astype(jnp.float32)).astype(jnp.bfloat16)
+            side[k, p] = send(
+                ysend.at[k, here], yrecv.at[k, here], ysend_sem.at[k, p], yrecv_sem.at[k, p], 2
+            )
+        own[k, 0:plane] = own[k, 0:plane] + crecv[k, 0:plane].astype(jnp.float32)
+
+    def start_line(k, dz, bit, value):
+        zsend[k, dz] = value.astype(jnp.bfloat16)
+        line[k, dz] = send(
+            zsend.at[k, dz], zrecv.at[k, dz], zsend_sem.at[k, dz], zrecv_sem.at[k, dz], 4 * bit
+        )
+
+    def finish_side(k):
+        for p in range(2):
+            side[k, p].wait_recv()
+            for dz in range(groups - 1 - p * groups // 2, groups // 2 - 1 - p * groups // 2, -1):
+                value = own[k, row_of(dz)] + yrecv[k, row_of(dz)].astype(jnp.float32)
+                if dz % 2:
+                    start_line(k, dz, 1, value)
+                else:
+                    own[k, row_of(dz)] = value
+
+    def finish_line(k, bit):
+        for dz in range(groups - 2 * bit, -1, -2 * bit):
+            line[k, dz + bit].wait_recv()
+            value = own[k, row_of(dz)] + zrecv[k, dz + bit].astype(jnp.float32)
+            if dz == 0 and 2 * bit == groups:
+                out_ref[k * part : (k + 1) * part] = value.astype(jnp.bfloat16)
+            elif dz % (4 * bit):
+                start_line(k, dz, 2 * bit, value)
+            else:
+                own[k, row_of(dz)] = value
+
+    levels = groups.bit_length() - 1
+    for turn in range(chunks + 1 + levels):
+        if turn < chunks:
+            multiply(turn)
+            finish_core(turn)
+        for level in range(levels - 1, -1, -1):
+            if 0 <= turn - 2 - level < chunks:
+                finish_line(turn - 2 - level, 1 << level)
+        if 0 <= turn - 1 < chunks:
+            finish_side(turn - 1)
+    for copies in (dispatch, core, side, line):
+        for copy in copies.values():
+            copy.wait_send()
+
+
+def scratch_of(n, tokens, chosen, features, width):
+    part = tokens // CHUNKS
+    plane = n // 4 * part
+    small = jnp.bfloat16
+    return [
+        ((tokens, chosen, 2 * features), small),
+        ((features, width), small),
+        ((CHUNKS, n * part, features), small),
+        ((CHUNKS, n * part, features), small),
+        ((CHUNKS, 2 * plane, width), jnp.float32),
+        ((CHUNKS, 2 * plane, width), small),
+        ((CHUNKS, 2 * plane, width), small),
+        ((CHUNKS, plane, width), small),
+        ((CHUNKS, plane, width), small),
+        ((CHUNKS, n // 4, part, width), small),
+        ((CHUNKS, n // 4, part, width), small),
+    ]
+
+
+def bytes_of(buffers):
+    total = 0
+    for shape, kind in buffers:
+        size = jnp.dtype(kind).itemsize
+        for extent in shape:
+            size *= extent
+        total += size
+    return total
+
+
+def on_device(expert_ids, route_gates, routed_in, down_weight, slot_offset):
+    n = lax.axis_size("ep")
+    tokens, chosen = expert_ids.shape
+    features, width = down_weight.shape[1:]
+    buffers = scratch_of(n, tokens, chosen, features, width)
+    if (
+        n < 8
+        or n & (n - 1)
+        or tokens % (16 * CHUNKS)
+        or chosen % 8
+        or features % TILE
+        or width % TILE
+        or bytes_of(buffers) > VMEM_LIMIT * 3 // 4
+    ):
+        return exchange_form(expert_ids, route_gates, routed_in, down_weight, slot_offset)
+    target = jnp.mod(expert_ids - slot_offset[0], n)
+    dma = pltpu.SemaphoreType.DMA
+    return pl.pallas_call(
+        functools.partial(kernel, n),
+        out_shape=jax.ShapeDtypeStruct((tokens, width), jnp.bfloat16),
+        in_specs=[pl.BlockSpec(memory_space=pltpu.VMEM)] * 2 + [pl.BlockSpec(memory_space=pl.ANY)] * 2,
+        out_specs=pl.BlockSpec(memory_space=pltpu.VMEM),
+        scratch_shapes=[pltpu.VMEM(shape, kind) for shape, kind in buffers]
+        + [dma((1,)), dma((CHUNKS,))]
+        + [dma((CHUNKS, n))] * 2
+        + [dma((CHUNKS,))] * 2
+        + [dma((CHUNKS, 2))] * 2
+        + [dma((CHUNKS, n // 4))] * 2,
+        compiler_params=pltpu.CompilerParams(
+            collective_id=0, has_side_effects=True, vmem_limit_bytes=VMEM_LIMIT
+        ),
+    )(target, route_gates, routed_in, down_weight)
+
+
 def solution(mesh):
     placed = (
         P(("grp", "ep"), None),

time: 262 us -> 96.5 us (0.37)
  the two profiles are of different devices: /device:TPU:13 before, /device:TPU:0 now
where the time goes in v2:
time: 96.5 us; the launch traced here: 96.3 us
  Pallas kernels  91 us (94%)
  local copies, waits for them, and re-layouts  3.96 us (4%)
    pallas_call x1, Pallas kernels, on_device(): pl.pallas_call(functools.partial(kernel, n), out_shape=jax.ShapeDtypeStru...  91 us
    unnamed x3, local copies, waits for them, and re-layouts  3.96 us

profile of v2, /device:TPU:0, one launch (start us, length us, event | category | flops | bytes accessed | tf_op | source)
XLA Modules:
  0.0 96.3 jit_solution(13687150649841386086)
XLA Ops:
  0.7 0.8 copy.6
  1.4 0.6 add_select_fusion.target_ref
  2.1 1.4 %copy.7.gate_ref = f32[64,8]{1,0:T(8,128)} copy(f32[64,8]{0,1:T(8,128)} %param.6) | data formatting | bytes 4096 | tf_op args[1]
  3.4 91.0 %shard_map.55 = bf16[64,3584]{1,0:T(8,128)(2,1)} custom-call(s32[64,8]{1,0:T(8,128)} %add_select_fusion.target_ref, f32[64,8]{1,0:T(8,128)} %copy.7.gate_ref, bf16[64,8,2048]{2,1,0:T(8,128)(2,1)} %x_hbm.1, bf16[1,1024,3584]{2,1,0:T(8,128)(2,1)} %w_hbm.1), custom_call_target="tpu_custom_call" | custom-call | tf_op jit(solution)/shard_map/pallas_call | solution.py:293
  94.4 1.8 %copy.10 = bf16[64,3584]{1,0:T(8,128)(2,1)} copy(bf16[64,3584]{1,0:T(8,128)(2,1)} %shard_map.55) | data formatting | bytes 917504

commit v3 on v2

--- a/solution.py
+++ b/solution.py
@@ -10,6 +10,7 @@
 MESH = pl.DeviceIdType.MESH
 TILE = 256
 CHUNKS = 4
+AHEAD = 3
 VMEM_LIMIT = 63 * 1024 * 1024
 
 
@@ -143,6 +144,15 @@
     slots = [slot_distance(n, s) for s in range(n)]
     peers = [flipped(me, d) for d in slots]
     dispatch = {}
+
+    def issue(k):
+        for d in range(1, n):
+            s = slots.index(d)
+            here = pl.ds(s * part, part)
+            dispatch[k, s] = send(
+                outg.at[k, here], recv.at[k, here], dsend_sem.at[k, s], drecv_sem.at[k, s], d
+            )
+
     for k in range(chunks):
         target = target_ref[k * part : (k + 1) * part]
         gates = gate_ref[k * part : (k + 1) * part]
@@ -164,12 +174,8 @@
                     recv[k, s * part : (s + 1) * part, c : c + TILE] = rows[s * part : (s + 1) * part]
         if k == 0:
             pl.semaphore_wait(barrier, n - 1)
-        for d in range(n - 1, 0, -1):
-            s = slots.index(d)
-            here = pl.ds(s * part, part)
-            dispatch[k, s] = send(
-                outg.at[k, here], recv.at[k, here], dsend_sem.at[k, s], drecv_sem.at[k, s], d
-            )
+        if k < AHEAD:
+            issue(k)
     w_copy.wait()
 
     core, side, line = {}, {}, {}
@@ -234,6 +240,8 @@
         if turn < chunks:
             multiply(turn)
             finish_core(turn)
+            if turn + AHEAD < chunks:
+                issue(turn + AHEAD)
         for level in range(levels - 1, -1, -1):
             if 0 <= turn - 2 - level < chunks:
                 finish_line(turn - 2 - level, 1 << level)

time: 96.5 us -> 95.3 us (0.988)
  Pallas kernels: 91 us -> 89.8 us
    pallas_call x1, Pallas kernels: 91 us -> 89.8 us  [on_device(): pl.pallas_call(functools.partial(kernel, n), out_shape=jax.ShapeDtypeStru...]
where the time goes in v3:
time: 95.3 us; the launch traced here: 95 us
  Pallas kernels  89.8 us (94%)
  local copies, waits for them, and re-layouts  3.96 us (4%)
    pallas_call x1, Pallas kernels, on_device(): pl.pallas_call(functools.partial(kernel, n), out_shape=jax.ShapeDtypeStru...  89.8 us
    unnamed x3, local copies, waits for them, and re-layouts  3.96 us

profile of v3, /device:TPU:0, one launch (start us, length us, event | category | flops | bytes accessed | tf_op | source)
XLA Modules:
  0.0 95.0 jit_solution(2034018637451555479)
XLA Ops:
  0.7 0.8 copy.6
  1.4 0.6 add_select_fusion.target_ref
  2.1 1.4 %copy.7.gate_ref = f32[64,8]{1,0:T(8,128)} copy(f32[64,8]{0,1:T(8,128)} %param.6) | data formatting | bytes 4096 | tf_op args[1]
  3.4 89.8 %shard_map.55 = bf16[64,3584]{1,0:T(8,128)(2,1)} custom-call(s32[64,8]{1,0:T(8,128)} %add_select_fusion.target_ref, f32[64,8]{1,0:T(8,128)} %copy.7.gate_ref, bf16[64,8,2048]{2,1,0:T(8,128)(2,1)} %x_hbm.1, bf16[1,1024,3584]{2,1,0:T(8,128)(2,1)} %w_hbm.1), custom_call_target="tpu_custom_call" | custom-call | tf_op jit(solution)/shard_map/pallas_call | solution.py:301
  93.2 1.8 %copy.10 = bf16[64,3584]{1,0:T(8,128)(2,1)} copy(bf16[64,3584]{1,0:T(8,128)(2,1)} %shard_map.55) | data formatting | bytes 917504
